TPU v7x, 256 devices: a whole 4x4x8 slice. The times are simulated.
256 devices in a mesh: pb: 64 (over x, y, z_hi, core), ga: 4 (over z_lo).
Axes of the slice: x: 4, y: 4, z: 8 (z_hi: 2, z_lo: 4; z = z_hi * 4 + z_lo), core: 2. Of those that a mesh axis runs over, the one named last changes fastest.
Arguments:
- query_points: float32 [3, 262144], P(None, 'pb'), may hold values from 0 to 1
- cotangent: bfloat16 [64, 262144], P(None, 'pb'), may hold values from -6 to 6
- slab_ids: int32 [8, 262144], P(None, 'pb'), may hold values from -1 to 3
- rel_cells: int32 [8, 262144], P(None, 'pb'), may hold values from 0 to 511
- offsets: int32 [4, 2048], P('ga', 'pb'), may hold values from 0 to 15872
- latent: bfloat16 [4, 64, 16384], P('ga', None, 'pb'), may hold values from -6 to 6
- w_in: float32 [80, 6], replicated, may hold values from -2.5 to 2.5
- b_in: float32 [80], replicated, may hold values from -3 to 3
- w_out: bfloat16 [64, 80], replicated, may hold values from -0.625 to 0.625
- b_out: float32 [64], replicated, may hold values from -3 to 3
Outputs:
- grid_grad: float32 [4, 64, 16384], P('ga', None, 'pb')
- w_in_grad: float32 [80, 6], replicated
- b_in_grad: float32 [80], replicated
- w_out_grad: float32 [64, 80], replicated
- b_out_grad: float32 [64], replicated
Inputs may be any that keep to these rules, and one draw needn't show every extreme that they name: `slab_ids`: -1 marks a padding slot; otherwise the slab that holds the neighbour cell.
All inputs are finite; a program needn't handle non-finite values.
Results may differ from a plain program's by a relative error of at most 0.0085.
Values may be sent and summed in bfloat16 or wider, within the bound.
A program may use at most 64 MiB of HBM per device.

v0:
```python
import functools
import math
import jax
import jax.numpy as jnp
from jax import lax
from jax.sharding import Mesh
from jax.sharding import PartitionSpec as P

KN = 8
TILE = 128
WIN = 512
GX = 64
ZS = 4
PB = ("pb_0", "pb_1", "pb_2", "pb_3")
PB_GA = ("pb_0", "pb_1", "pb_2", "pb_3", "ga")


def cut_along(value, dim, length):
    before, after = (value.shape[:dim], value.shape[dim + 1 :])
    return jnp.moveaxis(value.reshape(*before, length, -1, *after), dim, 0)


def sum_at_owner(value, axis, dim):
    tiles = cut_along(value, dim, lax.axis_size(axis))
    arrived = lax.all_to_all(tiles, axis, split_axis=0, concat_axis=0, tiled=True)
    return arrived.astype(jnp.float32).sum(axis=0)


def by_axis(value, axes):
    return functools.reduce(lax.psum, axes, value)


def gelu_exact(values):
    return jax.nn.gelu(values, approximate=False)


def shards(query_points, cotangent, slab_ids, rel_cells, offsets, latent, w_in, b_in, w_out, b_out):
    channels = latent.shape[1]
    slab_feats = lax.all_gather(latent, PB, axis=2, tiled=True)[0]
    cells_slab = slab_feats.shape[1]
    slab_here = lax.axis_index("ga")
    queries_dev = query_points.shape[1]
    tiles_dev = queries_dev // TILE
    per_block = math.gcd(tiles_dev, 4)
    blocks = tiles_dev // per_block
    entries = KN * TILE

    def reshape_tiles(values):
        leading = values.shape[0]
        return values.reshape(leading, blocks, per_block, TILE).transpose(1, 2, 0, 3)

    def tile_work(anchor, points, cot_cols, slabs, rels):
        window = lax.dynamic_slice_in_dim(slab_feats, anchor, WIN, 1)
        rel_flat = rels.reshape(-1)
        live_flat = slabs.reshape(-1) == slab_here
        onehot = (
            (lax.broadcasted_iota(jnp.int32, (WIN, entries), 0) == rel_flat[None, :])
            & live_flat[None, :]
        ).astype(jnp.bfloat16)
        feats = jnp.dot(window, onehot, preferred_element_type=jnp.float32)
        cell = anchor + rel_flat
        along_x = cell // (GX * ZS)
        along_y = cell // ZS % GX
        along_z = cell % ZS + slab_here * ZS
        centres = jnp.stack(
            [
                (along_x.astype(jnp.float32) + 0.5) / GX,
                (along_y.astype(jnp.float32) + 0.5) / GX,
                (along_z.astype(jnp.float32) + 0.5) / GX,
            ],
            0,
        )
        features_in = jnp.concatenate([jnp.tile(points, (1, KN)), centres], 0)
        mask_flat = live_flat.astype(jnp.float32)
        cot_flat = jnp.tile(cot_cols.astype(jnp.float32), (1, KN))
        preact = (
            jnp.dot(
                w_in,
                features_in,
                precision=lax.Precision.HIGHEST,
                preferred_element_type=jnp.float32,
            )
            + b_in[:, None]
        )
        hidden = gelu_exact(preact).astype(jnp.bfloat16)
        kernel = jnp.dot(w_out, hidden, preferred_element_type=jnp.float32) + b_out[:, None]
        grad_cell = (kernel * cot_flat * mask_flat).astype(jnp.bfloat16)
        grad_kernel = (feats * cot_flat * mask_flat).astype(jnp.bfloat16)
        window_grad = lax.dot_general(
            grad_cell, onehot, (((1,), (1,)), ((), ())), preferred_element_type=jnp.float32
        )
        grad_w_out = lax.dot_general(
            grad_kernel, hidden, (((1,), (1,)), ((), ())), preferred_element_type=jnp.float32
        )
        grad_b_out = jnp.sum(grad_kernel.astype(jnp.float32), 1)
        grad_hidden = lax.dot_general(
            w_out, grad_kernel, (((0,), (0,)), ((), ())), preferred_element_type=jnp.float32
        )
        grad_pre = jax.vjp(gelu_exact, preact)[1](grad_hidden)[0]
        grad_w_in = lax.dot_general(
            grad_pre,
            features_in,
            (((1,), (1,)), ((), ())),
            precision=lax.Precision.HIGHEST,
            preferred_element_type=jnp.float32,
        )
        grad_b_in = jnp.sum(grad_pre, 1)
        return (window_grad, grad_w_in, grad_b_in, grad_w_out, grad_b_out)

    def advance(running, inputs_block):
        partial_grad, totals = running
        anchors, points, cot_cols, slabs, rels = inputs_block
        results = jax.vmap(tile_work)(anchors, points, cot_cols, slabs, rels)
        for number in range(per_block):
            current = lax.dynamic_slice_in_dim(partial_grad, anchors[number], WIN, 1)
            partial_grad = lax.dynamic_update_slice_in_dim(
                partial_grad, current + results[0][number], anchors[number], 1
            )
        totals = tuple((old + jnp.sum(new, 0) for old, new in zip(totals, results[1:])))
        return ((partial_grad, totals), None)

    start_totals = (
        jnp.zeros((w_in.shape[0], 6), jnp.float32),
        jnp.zeros((w_in.shape[0],), jnp.float32),
        jnp.zeros((channels, w_in.shape[0]), jnp.float32),
        jnp.zeros((channels,), jnp.float32),
    )
    start_grid = jnp.zeros((channels, cells_slab), jnp.float32)
    inputs_all = (
        offsets[0].reshape(blocks, per_block),
        reshape_tiles(query_points),
        reshape_tiles(cotangent),
        reshape_tiles(slab_ids),
        reshape_tiles(rel_cells),
    )
    (partial_grad, totals), _ = lax.scan(advance, (start_grid, start_totals), inputs_all)
    owned = sum_at_owner(partial_grad.astype(jnp.bfloat16), PB, 1)
    sums = (
        by_axis(totals[0], PB_GA),
        by_axis(totals[1], PB_GA),
        by_axis(totals[2], PB_GA),
        by_axis(totals[3], PB_GA),
    )
    scale = float(queries_dev * lax.axis_size(PB)) ** (-0.5)
    return (owned[None], sums[0] * scale, sums[1] * scale, sums[2] * scale, sums[3] * scale)


def solution(mesh):
    finer = Mesh(
        mesh.devices.reshape(4, 4, 2, 2, mesh.shape["ga"]), ("pb_0", "pb_1", "pb_2", "pb_3", "ga")
    )
    in_specs = (
        P(None, PB),
        P(None, PB),
        P(None, PB),
        P(None, PB),
        P("ga", PB),
        P("ga", None, PB),
        P(),
        P(),
        P(),
        P(),
    )
    out_specs = (P("ga", None, PB), P(), P(), P(), P())
    return jax.shard_map(
        shards, mesh=finer, in_specs=in_specs, out_specs=out_specs, check_vma=False
    )
```

profile of v0, /device:TPU:2, one launch (start us, length us, event | category | flops | bytes accessed | tf_op | source)
XLA Modules:
  0.0 575.7 jit_solution(1907002252681811050)
XLA Ops:
  10.7 2.3 reshape.397
  13.0 86.1 %all-gather.2.cloned.1.call-done = bf16[1,64,16384]{2,1,0:T(8,128)(2,1)} async-done(((bf16[1,64,256]{2,1,0:T(8,128)(2,1)}), bf16[1,64,16384]{2,1,0:T(8,128)(2,1)}) %all-gather.2.cloned.1.call-update) | async-done | bytes 2097168 | tf_op jit(solution)/shard_map/all_gather | solution.py:39
  99.1 2.3 broadcast_in_dim.12
  101.4 365.0 %while.26 = (s32[]{:T(128)}, f32[64,16384]{1,0:T(8,128)}, f32[80,6]{0,1:T(8,128)S(1)}, f32[80]{0:T(128)S(1)}, f32[64,80]{1,0:T(8,128)S(1)}, /*index=5*/f32[64]{0...) while((s32[]{:T(128)}, f32[64,16384]{1,0:T(8,128)}, ...), condition=%wide.region_3.4_spmd.clone, body=%wide.region_0.3_spmd.clone.sunk | while | flops 747289728 | bytes 21654660 | solution.py:136
  112.4 8.9 %while.27 = (s32[]{:T(128)}, bf16[64,16384]{1,0:T(8,128)(2,1)}, s32[4,2]{0,1:T(2,128)S(1)}, bf16[4,64,512]{2,1,0:T(8,128)(2,1)S(1)}, s32[]{:T(128)}) while((s32[]{:T(128)}, bf16[64,16384]{1,0:T(8,128)(2,1)}, s32[4,2]{0,1:T(2,128)S(1)}, bf16[4,64,512]{2,1,0:T(8,128)(2,1)S(1)}, s32[]{:T(128)}) %tuple.83), condition=%wide.while_cond, body=%wide.while_body.sunk | while | flops 2 | bytes 131177 | solution.py:53
  123.8 5.4 fusion.121
  129.1 2.3 fusion.122
  131.4 2.6 fusion.128
  158.0 8.9 %while.27 = (s32[]{:T(128)}, bf16[64,16384]{1,0:T(8,128)(2,1)}, s32[4,2]{0,1:T(2,128)S(1)}, bf16[4,64,512]{2,1,0:T(8,128)(2,1)S(1)}, s32[]{:T(128)}) while((s32[]{:T(128)}, bf16[64,16384]{1,0:T(8,128)(2,1)}, s32[4,2]{0,1:T(2,128)S(1)}, bf16[4,64,512]{2,1,0:T(8,128)(2,1)S(1)}, s32[]{:T(128)}) %tuple.83), condition=%wide.while_cond, body=%wide.while_body.sunk | while | flops 2 | bytes 131177 | solution.py:53
  167.1 2.2 convert_reduce_fusion.3
  169.4 5.4 fusion.121
  174.7 2.3 fusion.122
  177.0 2.6 fusion.128
  203.6 8.9 %while.27 = (s32[]{:T(128)}, bf16[64,16384]{1,0:T(8,128)(2,1)}, s32[4,2]{0,1:T(2,128)S(1)}, bf16[4,64,512]{2,1,0:T(8,128)(2,1)S(1)}, s32[]{:T(128)}) while((s32[]{:T(128)}, bf16[64,16384]{1,0:T(8,128)(2,1)}, s32[4,2]{0,1:T(2,128)S(1)}, bf16[4,64,512]{2,1,0:T(8,128)(2,1)S(1)}, s32[]{:T(128)}) %tuple.83), condition=%wide.while_cond, body=%wide.while_body.sunk | while | flops 2 | bytes 131177 | solution.py:53
  215.0 5.4 fusion.121
  220.4 2.3 fusion.122
  222.7 2.6 fusion.128
  249.2 8.9 %while.27 = (s32[]{:T(128)}, bf16[64,16384]{1,0:T(8,128)(2,1)}, s32[4,2]{0,1:T(2,128)S(1)}, bf16[4,64,512]{2,1,0:T(8,128)(2,1)S(1)}, s32[]{:T(128)}) while((s32[]{:T(128)}, bf16[64,16384]{1,0:T(8,128)(2,1)}, s32[4,2]{0,1:T(2,128)S(1)}, bf16[4,64,512]{2,1,0:T(8,128)(2,1)S(1)}, s32[]{:T(128)}) %tuple.83), condition=%wide.while_cond, body=%wide.while_body.sunk | while | flops 2 | bytes 131177 | solution.py:53
  258.4 2.2 convert_reduce_fusion.3
  260.6 5.4 fusion.121
  266.0 2.3 fusion.122
  268.3 2.6 fusion.128
  294.8 8.9 %while.27 = (s32[]{:T(128)}, bf16[64,16384]{1,0:T(8,128)(2,1)}, s32[4,2]{0,1:T(2,128)S(1)}, bf16[4,64,512]{2,1,0:T(8,128)(2,1)S(1)}, s32[]{:T(128)}) while((s32[]{:T(128)}, bf16[64,16384]{1,0:T(8,128)(2,1)}, s32[4,2]{0,1:T(2,128)S(1)}, bf16[4,64,512]{2,1,0:T(8,128)(2,1)S(1)}, s32[]{:T(128)}) %tuple.83), condition=%wide.while_cond, body=%wide.while_body.sunk | while | flops 2 | bytes 131177 | solution.py:53
  304.0 2.2 convert_reduce_fusion.3
  306.3 5.4 fusion.121
  311.6 2.3 fusion.122
  313.9 2.6 fusion.128
  340.5 8.9 %while.27 = (s32[]{:T(128)}, bf16[64,16384]{1,0:T(8,128)(2,1)}, s32[4,2]{0,1:T(2,128)S(1)}, bf16[4,64,512]{2,1,0:T(8,128)(2,1)S(1)}, s32[]{:T(128)}) while((s32[]{:T(128)}, bf16[64,16384]{1,0:T(8,128)(2,1)}, s32[4,2]{0,1:T(2,128)S(1)}, bf16[4,64,512]{2,1,0:T(8,128)(2,1)S(1)}, s32[]{:T(128)}) %tuple.83), condition=%wide.while_cond, body=%wide.while_body.sunk | while | flops 2 | bytes 131177 | solution.py:53
  349.7 2.2 convert_reduce_fusion.3
  351.9 5.4 fusion.121
  357.3 2.3 fusion.122
  359.6 2.6 fusion.128
  386.1 8.9 %while.27 = (s32[]{:T(128)}, bf16[64,16384]{1,0:T(8,128)(2,1)}, s32[4,2]{0,1:T(2,128)S(1)}, bf16[4,64,512]{2,1,0:T(8,128)(2,1)S(1)}, s32[]{:T(128)}) while((s32[]{:T(128)}, bf16[64,16384]{1,0:T(8,128)(2,1)}, s32[4,2]{0,1:T(2,128)S(1)}, bf16[4,64,512]{2,1,0:T(8,128)(2,1)S(1)}, s32[]{:T(128)}) %tuple.83), condition=%wide.while_cond, body=%wide.while_body.sunk | while | flops 2 | bytes 131177 | solution.py:53
  397.6 5.4 fusion.121
  402.9 2.3 fusion.122
  405.2 2.6 fusion.128
  431.8 8.9 %while.27 = (s32[]{:T(128)}, bf16[64,16384]{1,0:T(8,128)(2,1)}, s32[4,2]{0,1:T(2,128)S(1)}, bf16[4,64,512]{2,1,0:T(8,128)(2,1)S(1)}, s32[]{:T(128)}) while((s32[]{:T(128)}, bf16[64,16384]{1,0:T(8,128)(2,1)}, s32[4,2]{0,1:T(2,128)S(1)}, bf16[4,64,512]{2,1,0:T(8,128)(2,1)S(1)}, s32[]{:T(128)}) %tuple.83), condition=%wide.while_cond, body=%wide.while_body.sunk | while | flops 2 | bytes 131177 | solution.py:53
  443.2 5.4 fusion.121
  448.5 2.3 fusion.122
  450.8 2.6 fusion.128
  466.4 2.4 convert_element_type.102
  469.4 2.5 copy.31
  471.9 6.8 %all-to-all-start = ((bf16[64,64,256]{2,1,0:T(8,128)(2,1)}), bf16[64,64,256]{2,1,0:T(8,128)(2,1)S(1)}, u32[]{:S(2)}, u32[]{:S(2)}) async-start(bf16[64,64,256]{2,1,0:T(8,128)(2,1)} %copy.31), calls=%async_computation | async-start | bytes 4194304 | tf_op jit(solution)/shard_map/all_to_all | solution.py:25
  478.7 29.5 %all-reduce.3 = (f32[80,6]{0,1:T(8,128)S(1)}, f32[80]{0:T(128)S(1)}, f32[64,80]{1,0:T(8,128)S(1)}, f32[64]{0:T(128)S(1)}) all-reduce(f32[80,6]{0,1:T(8,128)S(1)} %get-tuple-element.285, f32[80]{0:T(128)S(1)} %get-tuple-element.286, ...), channel_id=1, replica_groups=mesh['pb_0'=4,'pb_1'=4,'pb_2'=2,'pb_3'=2,'ga'=4] {'pb_0'}, use_global_device_ids=true, to_apply=%region_5.6 | all-reduce | flops 5744 | bytes 45952 | tf_op jit(solution)/shard_map/psum | solution.py:30
  508.2 17.2 %all-reduce.2 = (f32[80,6]{0,1:T(8,128)S(1)}, f32[80]{0:T(128)S(1)}, f32[64,80]{1,0:T(8,128)S(1)}, f32[64]{0:T(128)S(1)}) all-reduce(f32[80,6]{0,1:T(8,128)S(1)} %get-tuple-element.497, f32[80]{0:T(128)S(1)} %get-tuple-element.498, ...), channel_id=1, replica_groups=mesh['pb_0'=4,'pb_1'=4,'pb_2'=2,'pb_3'=2,'ga'=4] {'pb_1'}, use_global_device_ids=true, to_apply=%region_6.7 | all-reduce | flops 5744 | bytes 45952 | tf_op jit(solution)/shard_map/psum | solution.py:30
  525.4 20.7 %all-reduce.5 = (f32[80,6]{0,1:T(8,128)S(1)}, f32[80]{0:T(128)S(1)}, f32[64,80]{1,0:T(8,128)S(1)}, f32[64]{0:T(128)S(1)}) all-reduce(f32[80,6]{0,1:T(8,128)S(1)} %get-tuple-element.493, f32[80]{0:T(128)S(1)} %get-tuple-element.494, ...), channel_id=1, replica_groups=mesh['pb_0'=4,'pb_1'=4,'pb_2'=2,'pb_3'=2,'ga'=4] {'pb_2'}, use_global_device_ids=true, to_apply=%region_7.8 | all-reduce | flops 5744 | bytes 45952 | tf_op jit(solution)/shard_map/psum | solution.py:30
  546.1 3.5 all-reduce.4
  549.6 16.1 %all-reduce.1 = (f32[80,6]{0,1:T(8,128)S(1)}, f32[80]{0:T(128)S(1)}, f32[64,80]{1,0:T(8,128)S(1)}, f32[64]{0:T(128)S(1)}) all-reduce(f32[80,6]{0,1:T(8,128)S(1)} %get-tuple-element.501, f32[80]{0:T(128)S(1)} %get-tuple-element.502, ...), channel_id=1, replica_groups=mesh['pb_0'=4,'pb_1'=4,'pb_2'=2,'pb_3'=2,'ga'=4] {'ga'}, use_global_device_ids=true, to_apply=%region_9.10 | all-reduce | flops 5744 | bytes 45952 | tf_op jit(solution)/shard_map/psum | solution.py:30
  (373 shorter events, 218.3 us)
Async XLA Ops:
  7.2 91.9 %all-gather.2.cloned.1.call-start = ((), (), s32[]{:S(2)}) async-start(), calls=%async_computation.1 | async-start | bytes 2129920 | tf_op jit(solution)/shard_map/all_gather | solution.py:39
  99.1 2.3 copy-start
  99.1 2.3 copy-start.1
  99.1 2.3 copy-start.2
  99.1 2.3 copy-start.3
  471.9 96.0 %all-to-all-start = ((bf16[64,64,256]{2,1,0:T(8,128)(2,1)}), bf16[64,64,256]{2,1,0:T(8,128)(2,1)S(1)}, u32[]{:S(2)}, u32[]{:S(2)}) async-start(bf16[64,64,256]{2,1,0:T(8,128)(2,1)} %copy.31), calls=%async_computation | async-start | bytes 4194304 | tf_op jit(solution)/shard_map/all_to_all | solution.py:25
Sparse Core Ops, SparseCore 0:
  11.3 87.7 all-gather.1
where the time goes:
time: 581 us; the launch traced here: 576 us
  local copies, waits for them, and re-layouts  159 us (27%)
  matrix products  111 us (19%)
  blocking collectives  87 us (15%)
  waiting for transfers between devices  86.8 us (15%)
  loops' own time  63.4 us (11%)
  other arithmetic  47.1 us (8%)
  between operations  14.1 us (2%)
  starting transfers between devices  6.81 us (1%)
    psum x5, blocking collectives, by_axis(): return functools.reduce(lax.psum, axes, value)  87 us
    all_gather x1, waiting for transfers between devices, shards(): slab_feats = lax.all_gather(latent, PB, axis=2, tiled=True)[0]  86.1 us
    gather x96, local copies, waits for them, and re-layouts  70.8 us
    another operation x1, loops' own time, shards(): lax.scan(advance, (start_grid, start_totals), inputs_all)  62.7 us
    dynamic_update_slice x32, local copies, waits for them, and re-layouts, advance(): lax.dynamic_update_slice_in_dim(partial_grad, current + results[0][number...  59.4 us
    dot_general x8, matrix products, tile_work(): jnp.dot(w_in, features_in, precision=lax.Precision.HIGHEST, preferred_ele...  42.8 us
    add x32, other arithmetic, advance(): current + results[0][number]  32.5 us
    dot_general x8, matrix products, tile_work(): lax.dot_general(w_out, grad_kernel, (((0,), (0,)), ((), ())), preferred_e...  20.5 us
  transfers between devices with their start and end apart: 2, of which 1 were waited for; matrix products, arithmetic and copies ran while one was open for 1% of the time, Pallas kernels for 0%

commit v1 on v0

--- a/solution.py
+++ b/solution.py
@@ -13,6 +13,21 @@
 ZS = 4
 PB = ("pb_0", "pb_1", "pb_2", "pb_3")
 PB_GA = ("pb_0", "pb_1", "pb_2", "pb_3", "ga")
+
+
+def raise_the_field(x0, on_dim):
+    return jnp.concatenate(
+        lax.all_to_all(
+            jnp.stack([x0 for _ in range(lax.axis_size(PB))]),
+            axis_name=PB,
+            split_axis=0,
+            concat_axis=0,
+        ),
+        on_dim,
+    )
+
+
+manage_the_gates = functools.partial(raise_the_field, on_dim=2)
 
 
 def cut_along(value, dim, length):
@@ -36,7 +51,7 @@
 
 def shards(query_points, cotangent, slab_ids, rel_cells, offsets, latent, w_in, b_in, w_out, b_out):
     channels = latent.shape[1]
-    slab_feats = lax.all_gather(latent, PB, axis=2, tiled=True)[0]
+    slab_feats = manage_the_gates(latent)[0]
     cells_slab = slab_feats.shape[1]
     slab_here = lax.axis_index("ga")
     queries_dev = query_points.shape[1]

time: 581 us -> 543 us (0.935)
  waiting for transfers between devices: 86.8 us -> 36.1 us
  starting transfers between devices: 6.81 us -> 35.3 us
  between operations: 14.1 us -> 0.77 us
    all_gather x1 -> x0, waiting for transfers between devices: 86.1 us -> none  [shards(): slab_feats = lax.all_gather(latent, PB, axis=2, tiled=True)[0]]
    all_to_all x0 -> x1, waiting for transfers between devices: none -> 36.1 us  [raise_the_field(): lax.all_to_all(jnp.stack([x0 for _ in range(lax.axis_size(PB))]), axis_na...]
    all_to_all x0 -> x1, starting transfers between devices: none -> 14.8 us  [raise_the_field(): lax.all_to_all(jnp.stack([x0 for _ in range(lax.axis_size(PB))]), axis_na...]
    all_to_all x1, starting transfers between devices: 6.78 us -> 20.6 us  [sum_at_owner(): lax.all_to_all(tiles, axis, split_axis=0, concat_axis=0, tiled=True)]
    dynamic_slice x16, local copies, waits for them, and re-layouts: 12.7 us -> 6.02 us  [shards(): lax.scan(advance, (start_grid, start_totals), inputs_all)]
where the time goes in v1:
time: 543 us; the launch traced here: 538 us
  local copies, waits for them, and re-layouts  154 us (28%)
  matrix products  111 us (20%)
  blocking collectives  89.3 us (16%)
  loops' own time  63.6 us (12%)
  other arithmetic  46.9 us (9%)
  waiting for transfers between devices  36.1 us (7%)
  starting transfers between devices  35.3 us (7%)
    psum x5, blocking collectives, by_axis(): return functools.reduce(lax.psum, axes, value)  89.3 us
    gather x96, local copies, waits for them, and re-layouts  70.8 us
    another operation x1, loops' own time, shards(): lax.scan(advance, (start_grid, start_totals), inputs_all)  62.9 us
    dynamic_update_slice x32, local copies, waits for them, and re-layouts, advance(): lax.dynamic_update_slice_in_dim(partial_grad, current + results[0][number...  59.2 us
    dot_general x8, matrix products, tile_work(): jnp.dot(w_in, features_in, precision=lax.Precision.HIGHEST, preferred_ele...  42.9 us
    all_to_all x1, waiting for transfers between devices, raise_the_field(): lax.all_to_all(jnp.stack([x0 for _ in range(lax.axis_size(PB))]), axis_na...  36.1 us
    add x32, other arithmetic, advance(): current + results[0][number]  32.9 us
    all_to_all x1, starting transfers between devices, sum_at_owner(): lax.all_to_all(tiles, axis, split_axis=0, concat_axis=0, tiled=True)  20.6 us
  transfers between devices with their start and end apart: 2, of which 1 were waited for; matrix products, arithmetic and copies ran while one was open for 1% of the time, Pallas kernels for 0%

profile of v1, /device:TPU:2, one launch (start us, length us, event | category | flops | bytes accessed | tf_op | source)
XLA Modules:
  0.0 537.9 jit_solution(9319520927709773844)
XLA Ops:
  0.6 2.4 stack.8
  3.0 14.8 %all-to-all-start = ((bf16[64,1,64,256]{3,2,1,0:T(8,128)(2,1)}), bf16[64,1,64,256]{3,2,1,0:T(8,128)(2,1)S(1)}, u32[]{:S(2)}, u32[]{:S(2)}) async-start(bf16[64,1,64,256]{3,2,1,0:T(8,128)(2,1)} %stack.8), calls=%async_computation | async-start | bytes 4194304 | tf_op jit(solution)/shard_map/all_to_all | solution.py:20
  19.5 36.1 %all-to-all-done = bf16[64,1,64,256]{3,2,1,0:T(8,128)(2,1)S(1)} async-done(((bf16[64,1,64,256]{3,2,1,0:T(8,128)(2,1)}), bf16[64,1,64,256]{3,2,1,0:T(8,128)(2,1)S(1)}, u32[]{:S(2)}, u32[]{:S(2)}) %all-to-all-start) | async-done | bytes 2097184 | tf_op jit(solution)/shard_map/all_to_all | solution.py:20
  57.1 2.3 broadcast_in_dim.12
  59.4 359.9 %while.26 = (s32[]{:T(128)}, f32[64,16384]{1,0:T(8,128)}, f32[80,6]{0,1:T(8,128)S(1)}, f32[80]{0:T(128)S(1)}, f32[64,80]{1,0:T(8,128)S(1)}, /*index=5*/f32[64]{0...) while((s32[]{:T(128)}, f32[64,16384]{1,0:T(8,128)}, ...), condition=%wide.region_3.4_spmd.clone, body=%wide.region_0.3_spmd.clone.sunk | while | flops 747289728 | bytes 25849020 | solution.py:151
  69.7 8.9 %while.27 = (s32[]{:T(128)}, bf16[64,16384]{1,0:T(8,128)(2,1)}, s32[4,2]{0,1:T(2,128)S(1)}, bf16[4,64,512]{2,1,0:T(8,128)(2,1)S(1)}, s32[]{:T(128)}) while((s32[]{:T(128)}, bf16[64,16384]{1,0:T(8,128)(2,1)}, s32[4,2]{0,1:T(2,128)S(1)}, bf16[4,64,512]{2,1,0:T(8,128)(2,1)S(1)}, s32[]{:T(128)}) %tuple.83), condition=%wide.while_cond, body=%wide.while_body.sunk | while | flops 2 | bytes 131177 | solution.py:68
  81.1 5.4 fusion.121
  86.5 2.3 fusion.122
  88.8 2.6 fusion.128
  114.7 8.9 %while.27 = (s32[]{:T(128)}, bf16[64,16384]{1,0:T(8,128)(2,1)}, s32[4,2]{0,1:T(2,128)S(1)}, bf16[4,64,512]{2,1,0:T(8,128)(2,1)S(1)}, s32[]{:T(128)}) while((s32[]{:T(128)}, bf16[64,16384]{1,0:T(8,128)(2,1)}, s32[4,2]{0,1:T(2,128)S(1)}, bf16[4,64,512]{2,1,0:T(8,128)(2,1)S(1)}, s32[]{:T(128)}) %tuple.83), condition=%wide.while_cond, body=%wide.while_body.sunk | while | flops 2 | bytes 131177 | solution.py:68
  123.9 2.2 convert_reduce_fusion.3
  126.1 5.4 fusion.121
  131.5 2.3 fusion.122
  133.8 2.6 fusion.128
  159.7 8.9 %while.27 = (s32[]{:T(128)}, bf16[64,16384]{1,0:T(8,128)(2,1)}, s32[4,2]{0,1:T(2,128)S(1)}, bf16[4,64,512]{2,1,0:T(8,128)(2,1)S(1)}, s32[]{:T(128)}) while((s32[]{:T(128)}, bf16[64,16384]{1,0:T(8,128)(2,1)}, s32[4,2]{0,1:T(2,128)S(1)}, bf16[4,64,512]{2,1,0:T(8,128)(2,1)S(1)}, s32[]{:T(128)}) %tuple.83), condition=%wide.while_cond, body=%wide.while_body.sunk | while | flops 2 | bytes 131177 | solution.py:68
  168.9 2.2 convert_reduce_fusion.3
  171.1 5.4 fusion.121
  176.5 2.3 fusion.122
  178.8 2.6 fusion.128
  204.7 8.9 %while.27 = (s32[]{:T(128)}, bf16[64,16384]{1,0:T(8,128)(2,1)}, s32[4,2]{0,1:T(2,128)S(1)}, bf16[4,64,512]{2,1,0:T(8,128)(2,1)S(1)}, s32[]{:T(128)}) while((s32[]{:T(128)}, bf16[64,16384]{1,0:T(8,128)(2,1)}, s32[4,2]{0,1:T(2,128)S(1)}, bf16[4,64,512]{2,1,0:T(8,128)(2,1)S(1)}, s32[]{:T(128)}) %tuple.83), condition=%wide.while_cond, body=%wide.while_body.sunk | while | flops 2 | bytes 131177 | solution.py:68
  216.1 5.4 fusion.121
  221.4 2.3 fusion.122
  223.8 2.6 fusion.128
  249.7 8.9 %while.27 = (s32[]{:T(128)}, bf16[64,16384]{1,0:T(8,128)(2,1)}, s32[4,2]{0,1:T(2,128)S(1)}, bf16[4,64,512]{2,1,0:T(8,128)(2,1)S(1)}, s32[]{:T(128)}) while((s32[]{:T(128)}, bf16[64,16384]{1,0:T(8,128)(2,1)}, s32[4,2]{0,1:T(2,128)S(1)}, bf16[4,64,512]{2,1,0:T(8,128)(2,1)S(1)}, s32[]{:T(128)}) %tuple.83), condition=%wide.while_cond, body=%wide.while_body.sunk | while | flops 2 | bytes 131177 | solution.py:68
  261.1 5.4 fusion.121
  266.5 2.3 fusion.122
  268.8 2.6 fusion.128
  294.7 8.9 %while.27 = (s32[]{:T(128)}, bf16[64,16384]{1,0:T(8,128)(2,1)}, s32[4,2]{0,1:T(2,128)S(1)}, bf16[4,64,512]{2,1,0:T(8,128)(2,1)S(1)}, s32[]{:T(128)}) while((s32[]{:T(128)}, bf16[64,16384]{1,0:T(8,128)(2,1)}, s32[4,2]{0,1:T(2,128)S(1)}, bf16[4,64,512]{2,1,0:T(8,128)(2,1)S(1)}, s32[]{:T(128)}) %tuple.83), condition=%wide.while_cond, body=%wide.while_body.sunk | while | flops 2 | bytes 131177 | solution.py:68
  303.9 2.2 convert_reduce_fusion.3
  306.1 5.4 fusion.121
  311.5 2.3 fusion.122
  313.8 2.6 fusion.128
  339.7 8.9 %while.27 = (s32[]{:T(128)}, bf16[64,16384]{1,0:T(8,128)(2,1)}, s32[4,2]{0,1:T(2,128)S(1)}, bf16[4,64,512]{2,1,0:T(8,128)(2,1)S(1)}, s32[]{:T(128)}) while((s32[]{:T(128)}, bf16[64,16384]{1,0:T(8,128)(2,1)}, s32[4,2]{0,1:T(2,128)S(1)}, bf16[4,64,512]{2,1,0:T(8,128)(2,1)S(1)}, s32[]{:T(128)}) %tuple.83), condition=%wide.while_cond, body=%wide.while_body.sunk | while | flops 2 | bytes 131177 | solution.py:68
  351.1 5.4 fusion.121
  356.5 2.3 fusion.122
  358.8 2.6 fusion.128
  384.6 8.9 %while.27 = (s32[]{:T(128)}, bf16[64,16384]{1,0:T(8,128)(2,1)}, s32[4,2]{0,1:T(2,128)S(1)}, bf16[4,64,512]{2,1,0:T(8,128)(2,1)S(1)}, s32[]{:T(128)}) while((s32[]{:T(128)}, bf16[64,16384]{1,0:T(8,128)(2,1)}, s32[4,2]{0,1:T(2,128)S(1)}, bf16[4,64,512]{2,1,0:T(8,128)(2,1)S(1)}, s32[]{:T(128)}) %tuple.83), condition=%wide.while_cond, body=%wide.while_body.sunk | while | flops 2 | bytes 131177 | solution.py:68
  396.1 5.4 fusion.121
  401.4 2.3 fusion.122
  403.7 2.6 fusion.128
  419.3 2.4 convert_element_type.102
  422.3 2.5 copy.33
  424.8 20.6 %all-to-all-start.1 = ((bf16[64,64,256]{2,1,0:T(8,128)(2,1)}), bf16[64,64,256]{2,1,0:T(8,128)(2,1)S(1)}, u32[]{:S(2)}, u32[]{:S(2)}) async-start(bf16[64,64,256]{2,1,0:T(8,128)(2,1)} %copy.33), calls=%async_computation.1 | async-start | bytes 4194304 | tf_op jit(solution)/shard_map/all_to_all | solution.py:40
  445.4 29.7 %all-reduce.3 = (f32[80,6]{0,1:T(8,128)S(1)}, f32[80]{0:T(128)S(1)}, f32[64,80]{1,0:T(8,128)S(1)}, f32[64]{0:T(128)S(1)}) all-reduce(f32[80,6]{0,1:T(8,128)S(1)} %get-tuple-element.285, f32[80]{0:T(128)S(1)} %get-tuple-element.286, ...), channel_id=1, replica_groups=mesh['pb_0'=4,'pb_1'=4,'pb_2'=2,'pb_3'=2,'ga'=4] {'pb_0'}, use_global_device_ids=true, to_apply=%region_5.6 | all-reduce | flops 5744 | bytes 45952 | tf_op jit(solution)/shard_map/psum | solution.py:45
  475.0 17.7 %all-reduce.2 = (f32[80,6]{0,1:T(8,128)S(1)}, f32[80]{0:T(128)S(1)}, f32[64,80]{1,0:T(8,128)S(1)}, f32[64]{0:T(128)S(1)}) all-reduce(f32[80,6]{0,1:T(8,128)S(1)} %get-tuple-element.497, f32[80]{0:T(128)S(1)} %get-tuple-element.498, ...), channel_id=1, replica_groups=mesh['pb_0'=4,'pb_1'=4,'pb_2'=2,'pb_3'=2,'ga'=4] {'pb_1'}, use_global_device_ids=true, to_apply=%region_6.7 | all-reduce | flops 5744 | bytes 45952 | tf_op jit(solution)/shard_map/psum | solution.py:45
  492.7 20.5 %all-reduce.5 = (f32[80,6]{0,1:T(8,128)S(1)}, f32[80]{0:T(128)S(1)}, f32[64,80]{1,0:T(8,128)S(1)}, f32[64]{0:T(128)S(1)}) all-reduce(f32[80,6]{0,1:T(8,128)S(1)} %get-tuple-element.493, f32[80]{0:T(128)S(1)} %get-tuple-element.494, ...), channel_id=1, replica_groups=mesh['pb_0'=4,'pb_1'=4,'pb_2'=2,'pb_3'=2,'ga'=4] {'pb_2'}, use_global_device_ids=true, to_apply=%region_7.8 | all-reduce | flops 5744 | bytes 45952 | tf_op jit(solution)/shard_map/psum | solution.py:45
  513.3 3.5 all-reduce.4
  516.7 17.9 %all-reduce.1 = (f32[80,6]{0,1:T(8,128)S(1)}, f32[80]{0:T(128)S(1)}, f32[64,80]{1,0:T(8,128)S(1)}, f32[64]{0:T(128)S(1)}) all-reduce(f32[80,6]{0,1:T(8,128)S(1)} %get-tuple-element.501, f32[80]{0:T(128)S(1)} %get-tuple-element.502, ...), channel_id=1, replica_groups=mesh['pb_0'=4,'pb_1'=4,'pb_2'=2,'pb_3'=2,'ga'=4] {'ga'}, use_global_device_ids=true, to_apply=%region_9.10 | all-reduce | flops 5744 | bytes 45952 | tf_op jit(solution)/shard_map/psum | solution.py:45
  (412 shorter events, 214.8 us)
Async XLA Ops:
  3.0 15.4 %copy-start.6 = (s32[1,32]{1,0:T(1,128)S(1)}, s32[1,32]{1,0:T(1,128)}, u32[]{:S(2)}) copy-start(s32[1,32]{1,0:T(1,128)} %param.16) | copy-start | bytes 388
  3.0 16.1 %copy-start.3 = (f32[3,4096]{1,0:T(4,128)S(1)}, f32[3,4096]{1,0:T(4,128)}, u32[]{:S(2)}) copy-start(f32[3,4096]{1,0:T(4,128)} %param.12) | copy-start | bytes 147460
  3.0 16.2 %copy-start.2 = (bf16[64,4096]{1,0:T(8,128)(2,1)S(1)}, bf16[64,4096]{1,0:T(8,128)(2,1)}, u32[]{:S(2)}) copy-start(bf16[64,4096]{1,0:T(8,128)(2,1)} %param.13) | copy-start | bytes 1572868
  3.0 52.7 %all-to-all-start = ((bf16[64,1,64,256]{3,2,1,0:T(8,128)(2,1)}), bf16[64,1,64,256]{3,2,1,0:T(8,128)(2,1)S(1)}, u32[]{:S(2)}, u32[]{:S(2)}) async-start(bf16[64,1,64,256]{3,2,1,0:T(8,128)(2,1)} %stack.8), calls=%async_computation | async-start | bytes 4194304 | tf_op jit(solution)/shard_map/all_to_all | solution.py:20
  57.1 2.3 copy-start.4
  57.1 2.3 copy-start.5
  57.1 2.3 copy-start.7
  57.1 2.3 copy-start.8
  59.4 19.2 %copy-start = (bf16[8,4,64,128]{3,1,0,2:T(4,128)(2,1)}, bf16[8,4,64,128]{3,1,0,2:T(4,128)(2,1)S(1)}, u32[]{:S(2)}) copy-start(bf16[8,4,64,128]{3,1,0,2:T(4,128)(2,1)S(1)} %get-tuple-element.781) | copy-start | bytes 1572868 | tf_op jit(solution)/shard_map/while
  92.9 11.6 %copy-start.1 = (bf16[8,4,64,128]{3,1,0,2:T(4,128)(2,1)S(1)}, bf16[8,4,64,128]{3,1,0,2:T(4,128)(2,1)}, u32[]{:S(2)}) copy-start(bf16[8,4,64,128]{3,1,0,2:T(4,128)(2,1)} %copy-done) | copy-start | bytes 1572868 | tf_op jit(solution)/shard_map/while
  104.5 19.2 %copy-start = (bf16[8,4,64,128]{3,1,0,2:T(4,128)(2,1)}, bf16[8,4,64,128]{3,1,0,2:T(4,128)(2,1)S(1)}, u32[]{:S(2)}) copy-start(bf16[8,4,64,128]{3,1,0,2:T(4,128)(2,1)S(1)} %get-tuple-element.781) | copy-start | bytes 1572868 | tf_op jit(solution)/shard_map/while
  137.9 11.6 %copy-start.1 = (bf16[8,4,64,128]{3,1,0,2:T(4,128)(2,1)S(1)}, bf16[8,4,64,128]{3,1,0,2:T(4,128)(2,1)}, u32[]{:S(2)}) copy-start(bf16[8,4,64,128]{3,1,0,2:T(4,128)(2,1)} %copy-done) | copy-start | bytes 1572868 | tf_op jit(solution)/shard_map/while
  149.5 19.2 %copy-start = (bf16[8,4,64,128]{3,1,0,2:T(4,128)(2,1)}, bf16[8,4,64,128]{3,1,0,2:T(4,128)(2,1)S(1)}, u32[]{:S(2)}) copy-start(bf16[8,4,64,128]{3,1,0,2:T(4,128)(2,1)S(1)} %get-tuple-element.781) | copy-start | bytes 1572868 | tf_op jit(solution)/shard_map/while
  182.9 11.5 %copy-start.1 = (bf16[8,4,64,128]{3,1,0,2:T(4,128)(2,1)S(1)}, bf16[8,4,64,128]{3,1,0,2:T(4,128)(2,1)}, u32[]{:S(2)}) copy-start(bf16[8,4,64,128]{3,1,0,2:T(4,128)(2,1)} %copy-done) | copy-start | bytes 1572868 | tf_op jit(solution)/shard_map/while
  194.4 19.2 %copy-start = (bf16[8,4,64,128]{3,1,0,2:T(4,128)(2,1)}, bf16[8,4,64,128]{3,1,0,2:T(4,128)(2,1)S(1)}, u32[]{:S(2)}) copy-start(bf16[8,4,64,128]{3,1,0,2:T(4,128)(2,1)S(1)} %get-tuple-element.781) | copy-start | bytes 1572868 | tf_op jit(solution)/shard_map/while
  227.8 11.6 %copy-start.1 = (bf16[8,4,64,128]{3,1,0,2:T(4,128)(2,1)S(1)}, bf16[8,4,64,128]{3,1,0,2:T(4,128)(2,1)}, u32[]{:S(2)}) copy-start(bf16[8,4,64,128]{3,1,0,2:T(4,128)(2,1)} %copy-done) | copy-start | bytes 1572868 | tf_op jit(solution)/shard_map/while
  239.4 19.2 %copy-start = (bf16[8,4,64,128]{3,1,0,2:T(4,128)(2,1)}, bf16[8,4,64,128]{3,1,0,2:T(4,128)(2,1)S(1)}, u32[]{:S(2)}) copy-start(bf16[8,4,64,128]{3,1,0,2:T(4,128)(2,1)S(1)} %get-tuple-element.781) | copy-start | bytes 1572868 | tf_op jit(solution)/shard_map/while
  272.9 11.6 %copy-start.1 = (bf16[8,4,64,128]{3,1,0,2:T(4,128)(2,1)S(1)}, bf16[8,4,64,128]{3,1,0,2:T(4,128)(2,1)}, u32[]{:S(2)}) copy-start(bf16[8,4,64,128]{3,1,0,2:T(4,128)(2,1)} %copy-done) | copy-start | bytes 1572868 | tf_op jit(solution)/shard_map/while
  284.5 19.2 %copy-start = (bf16[8,4,64,128]{3,1,0,2:T(4,128)(2,1)}, bf16[8,4,64,128]{3,1,0,2:T(4,128)(2,1)S(1)}, u32[]{:S(2)}) copy-start(bf16[8,4,64,128]{3,1,0,2:T(4,128)(2,1)S(1)} %get-tuple-element.781) | copy-start | bytes 1572868 | tf_op jit(solution)/shard_map/while
  317.9 11.6 %copy-start.1 = (bf16[8,4,64,128]{3,1,0,2:T(4,128)(2,1)S(1)}, bf16[8,4,64,128]{3,1,0,2:T(4,128)(2,1)}, u32[]{:S(2)}) copy-start(bf16[8,4,64,128]{3,1,0,2:T(4,128)(2,1)} %copy-done) | copy-start | bytes 1572868 | tf_op jit(solution)/shard_map/while
  329.4 19.2 %copy-start = (bf16[8,4,64,128]{3,1,0,2:T(4,128)(2,1)}, bf16[8,4,64,128]{3,1,0,2:T(4,128)(2,1)S(1)}, u32[]{:S(2)}) copy-start(bf16[8,4,64,128]{3,1,0,2:T(4,128)(2,1)S(1)} %get-tuple-element.781) | copy-start | bytes 1572868 | tf_op jit(solution)/shard_map/while
  362.8 11.5 %copy-start.1 = (bf16[8,4,64,128]{3,1,0,2:T(4,128)(2,1)S(1)}, bf16[8,4,64,128]{3,1,0,2:T(4,128)(2,1)}, u32[]{:S(2)}) copy-start(bf16[8,4,64,128]{3,1,0,2:T(4,128)(2,1)} %copy-done) | copy-start | bytes 1572868 | tf_op jit(solution)/shard_map/while
  374.4 19.2 %copy-start = (bf16[8,4,64,128]{3,1,0,2:T(4,128)(2,1)}, bf16[8,4,64,128]{3,1,0,2:T(4,128)(2,1)S(1)}, u32[]{:S(2)}) copy-start(bf16[8,4,64,128]{3,1,0,2:T(4,128)(2,1)S(1)} %get-tuple-element.781) | copy-start | bytes 1572868 | tf_op jit(solution)/shard_map/while
  407.8 11.5 %copy-start.1 = (bf16[8,4,64,128]{3,1,0,2:T(4,128)(2,1)S(1)}, bf16[8,4,64,128]{3,1,0,2:T(4,128)(2,1)}, u32[]{:S(2)}) copy-start(bf16[8,4,64,128]{3,1,0,2:T(4,128)(2,1)} %copy-done) | copy-start | bytes 1572868 | tf_op jit(solution)/shard_map/while
  424.8 112.1 %all-to-all-start.1 = ((bf16[64,64,256]{2,1,0:T(8,128)(2,1)}), bf16[64,64,256]{2,1,0:T(8,128)(2,1)S(1)}, u32[]{:S(2)}, u32[]{:S(2)}) async-start(bf16[64,64,256]{2,1,0:T(8,128)(2,1)} %copy.33), calls=%async_computation.1 | async-start | bytes 4194304 | tf_op jit(solution)/shard_map/all_to_all | solution.py:40
